TPU v7x, 128 devices: a whole 4x4x4 slice. The times are simulated.
128 devices in a mesh: band: 128 (over z, y, x, core).
Axes of the slice: x: 4, y: 4, z: 4, core: 2. Of those that a mesh axis runs over, the one named last changes fastest.
Arguments:
- orbitals: float32 [128, 64, 4096], P('band'), may hold values from -6 to 6
- kernel_values: float32 [32], replicated, may hold values from 0.2 to 4
- shell_index: int32 [64, 4096], replicated, may hold values from 0 to 31, as said below
Outputs:
- exchange_term: float32 [128, 64, 4096], P('band')
- margin: float32 [128, 128], P('band')
Inputs may be any that keep to these rules, and one draw needn't show every extreme that they name: `shell_index`: the class of a wave vector is unchanged when any one of its indices a is replaced by (64 - a) mod 64.
All inputs are finite; a program needn't handle non-finite values.
Results may differ from a plain program's by a relative error of at most 0.0003.
Values sent between devices are 32-bit elements; how exact they have to be, the bound alone decides.
A program may use at most 64 MiB of HBM per device.

v0:
```python
import math

import jax
import jax.numpy as jnp
from jax import lax
from jax.sharding import Mesh
from jax.sharding import PartitionSpec as P

STEPS = 2
BAND = ("band_0", "band_1", "band_2", "band_3")


highest = lax.Precision.HIGHEST


def from_behind(value, axis, steps):
    count = lax.axis_size(axis)
    pairs = [(source, (source + steps) % count) for source in range(count)]
    return lax.ppermute(value, axis, pairs)


def cut_along(value, dim, size):
    before, after = (value.shape[:dim], value.shape[dim + 1 :])
    return jnp.moveaxis(value.reshape(*before, size, -1, *after), dim, 0)


def summed_on_arrival(value, axis, dim):
    parts = cut_along(value, dim, lax.axis_size(axis))
    arrived = lax.all_to_all(parts, axis, split_axis=0, concat_axis=0, tiled=True)
    return arrived.sum(axis=0)


def sum_by_axis(value, axes, dim):
    far, near = axes
    parts = cut_along(value, dim, lax.axis_size(far))
    nearer = summed_on_arrival(parts, near, dim + 1)
    arrived = lax.all_to_all(nearer, far, split_axis=0, concat_axis=0, tiled=True)
    return arrived.sum(axis=0)


def cas_matrix(extent):
    row_index = lax.broadcasted_iota(jnp.int32, (extent, extent), 0)
    col_index = lax.broadcasted_iota(jnp.int32, (extent, extent), 1)
    angle = 2.0 * math.pi / extent * (row_index * col_index % extent).astype(jnp.float32)
    return jnp.cos(angle) + jnp.sin(angle)


def block_table(table):
    extent = table.shape[0]
    copies = 128 // extent
    row_index = lax.broadcasted_iota(jnp.int32, (128, 128), 0)
    col_index = lax.broadcasted_iota(jnp.int32, (128, 128), 1)
    same_block = row_index // extent == col_index // extent
    tiled = jnp.tile(table, (copies, copies))
    return jnp.where(same_block, tiled, jnp.zeros_like(tiled))


def lookup(shell_index, kernel_values):
    classes = kernel_values.shape[0]

    def one_plane(indices):
        onehot = (indices[:, None] == jnp.arange(classes, dtype=jnp.int32)[None]).astype(
            jnp.float32
        )
        return jnp.dot(onehot, kernel_values, precision=highest, preferred_element_type=jnp.float32)

    return lax.map(one_plane, shell_index)


def transform(fields, table, wide_table):
    extent = table.shape[0]
    batch_rows = fields.shape[0]
    first_pass = jnp.einsum("ax,nxw->naw", table, fields, precision=highest)
    lanes = first_pass.reshape(batch_rows * extent * extent * extent // 128, 128)
    third_pass = jnp.dot(lanes, wide_table, precision=highest, preferred_element_type=jnp.float32)
    planes = third_pass.reshape(batch_rows * extent, extent, extent)
    second_pass = jnp.einsum("by,myz->mbz", table, planes, precision=highest)
    return second_pass.reshape(batch_rows, extent, extent * extent)


def potentials(left, right, kernel, table, wide_table):
    left_count = left.shape[0]
    right_count = right.shape[0]
    extent = table.shape[0]
    density = (left[:, None] * right[None]).reshape(
        left_count * right_count, extent, extent * extent
    )
    spectrum = transform(density, table, wide_table) * kernel[None]
    fields = transform(spectrum, table, wide_table) / float(extent**3)
    return fields.reshape(left_count, right_count, extent, extent * extent)


def local(orbitals, kernel_values, shell_index):
    extent = shell_index.shape[0]
    volume = extent**3
    table = cas_matrix(extent)
    wide_table = block_table(table)
    kernel = lookup(shell_index, kernel_values)
    local_count = orbitals.shape[0]
    flat_orbitals = orbitals.reshape(local_count, volume)
    grid_orbitals = lax.all_to_all(flat_orbitals, BAND, split_axis=1, concat_axis=0, tiled=True)
    own_fields = potentials(orbitals, orbitals, kernel, table, wide_table)
    exchange_term = -jnp.sum(own_fields * orbitals[None], axis=1)
    ahead_source = orbitals
    for distance in range(1, STEPS + 1):
        ahead_source = orbitals
        ahead_block = from_behind(ahead_source, BAND, distance)
        ahead_source = ahead_block
        pair_fields = potentials(orbitals, ahead_block, kernel, table, wide_table)
        exchange_term = exchange_term - jnp.sum(pair_fields * ahead_block[None], axis=1)
        sent_back = -jnp.sum(pair_fields * orbitals[:, None], axis=0)
        exchange_term = exchange_term + from_behind(sent_back, BAND, -distance)
    flat_terms = exchange_term.reshape(local_count, volume)
    grid_terms = lax.all_to_all(flat_terms, BAND, split_axis=1, concat_axis=0, tiled=True)
    margin = sum_by_axis(
        lax.dot_general(
            grid_orbitals,
            grid_terms,
            (((1,), (1,)), ((), ())),
            precision=highest,
            preferred_element_type=jnp.float32,
        ),
        (("band_0", "band_1", "band_2"), "band_3"),
        0,
    ) / float(volume)
    return (exchange_term, margin)


def solution(mesh):
    torus = Mesh(mesh.devices.reshape(4, 4, 4, 2), ("band_0", "band_1", "band_2", "band_3"))
    return jax.shard_map(
        local,
        mesh=torus,
        in_specs=(P(BAND, None, None), P(), P()),
        out_specs=(P(BAND, None, None), P(BAND, None)),
        check_vma=False,
    )
```

profile of v0, /device:TPU:1, one launch (start us, length us, event | category | flops | bytes accessed | tf_op | source)
XLA Modules:
  0.0 320.8 jit_solution(12334359458049599935)
XLA Ops:
  0.6 2.1 collective-permute-start.2
  2.7 2.1 collective-permute-start
  4.8 3.5 %all_to_all.33 = f32[1,128,2048]{2,0,1:T(1,128)} reshape(f32[1,64,4096]{2,1,0:T(8,128)} %param.5) | data formatting | bytes 2097152 | tf_op jit(solution)/shard_map/all_to_all | solution.py:101
  8.3 10.7 %all-to-all-start.1 = ((f32[1,128,2048]{2,0,1:T(1,128)}), f32[1,128,2048]{2,0,1:T(1,128)}, u32[]{:S(2)}, u32[]{:S(2)}) async-start(f32[1,128,2048]{2,0,1:T(1,128)} %all_to_all.33), calls=%async_computation.1 | async-start | bytes 2097152 | tf_op jit(solution)/shard_map/all_to_all | solution.py:101
  19.1 103.3 %while.10 = (s32[]{:T(128)}, f32[64,4096]{1,0:T(8,128)S(1)}, s32[64,4096]{1,0:T(8,128)}, f32[32]{0:T(128)S(1)}, s32[]{:T(128)}, /*index=5*/s32[]{:T(128)}) while((s32[]{:T(128)}, f32[64,4096]{1,0:T(8,128)S(1)}, s32[64,4096]{1,0:T(8,128)}, f32[32]{0:T(128)S(1)}, s32[]{:T(128)}, /*index=5*/s32[]{:T(128)}) %tuple.27), condition=%wide.region_1.2_spmd, body=%wide.region_0.1_spmd.sunk | while | flops 1703938 | bytes 98517 | solution.py:67
  20.7 0.9 constant_dynamic-slice_fusion.2
  28.7 0.9 constant_dynamic-slice_fusion.2
  35.2 0.9 constant_dynamic-slice_fusion.2
  36.8 0.9 constant_dynamic-slice_fusion.2
  43.3 0.9 constant_dynamic-slice_fusion.2
  51.3 0.9 constant_dynamic-slice_fusion.2
  59.4 0.9 constant_dynamic-slice_fusion.2
  65.9 0.9 constant_dynamic-slice_fusion.2
  123.3 2.2 convolution_bitcast_fusion.5
  125.4 2.3 reshape.1031
  127.8 3.2 fusion.78
  130.9 2.7 reshape.1032
  133.7 2.2 convolution_bitcast_fusion.1
  135.9 2.4 reshape.1043
  138.2 3.2 fusion.82
  141.4 2.7 reshape.1044
  144.1 6.3 %convolution_bitcast_fusion.6 = f32[64,64,64]{1,2,0:T(8,128)} fusion(f32[64,64,64]{2,1,0:T(8,128)} %reshape.1044), kind=kOutput, calls=%fused_computation.14 | convolution fusion | flops 201388032 | bytes 2097152 | tf_op jit(solution)/shard_map/by,myz->mbz/dot_general | solution.py:77
  150.4 2.9 copy.46
  153.3 2.3 reshape.1045
  155.7 2.2 convolution_bitcast_fusion
  157.9 2.4 reshape.1046
  160.2 2.2 fusion.83
  162.4 1.7 reshape.1047
  164.1 6.3 %multiply_bitcast_fusion = f32[64,64,64]{1,2,0:T(8,128)} fusion(f32[64,64,64]{2,1,0:T(8,128)} %reshape.1047), kind=kOutput, calls=%fused_computation.11 | convolution fusion | flops 201650176 | bytes 2097152 | tf_op jit(solution)/shard_map/by,myz->mbz/dot_general | solution.py:77
  170.4 2.9 copy.48
  173.4 2.1 div.61
  175.5 3.4 %convolution_bitcast_fusion.3 = f32[1,64,4096]{2,1,0:T(8,128)} fusion(f32[1,64,4096]{2,1,0:T(8,128)S(1)} %copy-done, f32[1,64,4096]{2,1,0:T(8,128)} %collective-permute-done), kind=kOutput, calls=%fused_computation.8 | convolution fusion | flops 201650176 | bytes 3145728 | tf_op jit(solution)/shard_map/ax,nxw->naw/dot_general | solution.py:73
  178.9 2.4 reshape.1037
  181.3 3.2 fusion.80
  184.5 3.1 reshape.1038
  187.5 6.3 %convolution_bitcast_fusion.7 = f32[64,64,64]{1,2,0:T(8,128)} fusion(f32[64,64,64]{2,1,0:T(8,128)} %reshape.1038), kind=kOutput, calls=%fused_computation.15 | convolution fusion | flops 201388032 | bytes 2097152 | tf_op jit(solution)/shard_map/by,myz->mbz/dot_general | solution.py:77
  193.9 2.9 copy.42
  196.8 2.9 reshape.1039
  199.7 3.4 %convolution_bitcast_fusion.2 = f32[1,64,4096]{2,1,0:T(8,128)} fusion(f32[64,4096]{1,0:T(8,128)} %reshape.1039, f32[64,4096]{1,0:T(8,128)S(1)} %get-tuple-element.24), kind=kOutput, calls=%fused_computation.7 | convolution fusion | flops 201650176 | bytes 3145728 | tf_op jit(solution)/shard_map/ax,nxw->naw/dot_general | solution.py:73
  203.1 2.4 reshape.1040
  205.5 2.2 fusion.81
  207.7 1.7 reshape.1041
  209.3 6.3 %multiply_bitcast_fusion.1 = f32[64,64,64]{1,2,0:T(8,128)} fusion(f32[64,64,64]{2,1,0:T(8,128)} %reshape.1041), kind=kOutput, calls=%fused_computation.12 | convolution fusion | flops 201650176 | bytes 2097152 | tf_op jit(solution)/shard_map/by,myz->mbz/dot_general | solution.py:77
  215.7 2.9 copy.44
  218.6 2.3 div.58
  220.9 1.5 multiply_negate_fusion.1
  222.5 1.0 collective-permute-start.1
  223.4 7.1 %collective-permute-start.3 = (f32[1,64,4096]{2,1,0:T(8,128)}, f32[1,64,4096]{2,1,0:T(8,128)}, u32[]{:S(2)}, u32[]{:S(2)}) collective-permute-start(f32[1,64,4096]{2,1,0:T(8,128)} %get-tuple-element.34), channel_id=1, source_target_pairs={{0,126},{1,127},{2,0},{3,1},{4,2},{5,3},{6,4},{7,5},{8,6},{9,7},{1... | collective-permute-start | bytes 3145736 | tf_op jit(solution)/shard_map/ppermute | solution.py:19
  230.6 4.9 %convolution_bitcast_fusion.8 = f32[64,64,64]{1,2,0:T(8,128)} fusion(f32[64,64,64]{2,1,0:T(8,128)S(1)} %copy-done.2), kind=kOutput, calls=%fused_computation.16 | convolution fusion | flops 201388032 | bytes 2097152 | tf_op jit(solution)/shard_map/by,myz->mbz/dot_general | solution.py:77
  235.4 2.9 copy.38
  238.4 2.9 reshape.1033
  241.3 3.8 %convolution_bitcast_fusion.4 = f32[1,64,4096]{2,1,0:T(8,128)} fusion(f32[64,4096]{1,0:T(8,128)} %reshape.1033, f32[64,4096]{1,0:T(8,128)} %copy-done.1), kind=kOutput, calls=%fused_computation.9 | convolution fusion | flops 201650176 | bytes 3145728 | tf_op jit(solution)/shard_map/ax,nxw->naw/dot_general | solution.py:73
  245.0 2.4 reshape.1034
  247.4 3.2 fusion.79
  250.6 2.7 reshape.1035
  253.3 6.3 %multiply_bitcast_fusion.2 = f32[64,64,64]{1,2,0:T(8,128)} fusion(f32[64,64,64]{2,1,0:T(8,128)} %reshape.1035), kind=kOutput, calls=%fused_computation.13 | convolution fusion | flops 201650176 | bytes 2097152 | tf_op jit(solution)/shard_map/by,myz->mbz/dot_general | solution.py:77
  259.6 2.9 copy.40
  262.5 2.9 div.55
  265.5 4.0 %subtract_add_fusion = f32[1,64,4096]{2,1,0:T(8,128)} fusion(f32[1,64,4096]{2,1,0:T(8,128)} %collective-permute-done.3, f32[1,64,4096]{2,1,0:T(8,128)S(1)} %div.61, f32[1,64,4096]{2,1,0:T(8,128)} %copy-done.3, f32[1,64,4096]{2,1,0:T(8,128)} %collective-permute-done.1, f32[1,64,4096]{2,1,0:T(8,128)S(1)} %div.58, f32[1,64,4096]{2,1,0:T(8,128)} %collective-permute-done, ...), kind=kLoop, calls=%fused_computation.26 | loop fusion | flops 2097152 | bytes 9437184 | tf_op jit(solution)/shard_map/add | solution.py:112
  269.5 2.5 all_to_all.38
  272.0 28.1 %all_to_all.43 = f32[1,128,2048]{2,0,1:T(1,128)S(1)} all-to-all(f32[1,128,2048]{2,0,1:T(1,128)S(1)} %all_to_all.38), channel_id=1, replica_groups=mesh['band_0'=4,'band_1'=4,'band_2'=4,'band_3'=2] {'band_0','band_1','ba..., dimensions={1} | all-to-all | bytes 2097152 | tf_op jit(solution)/shard_map/all_to_all | solution.py:114
  300.0 2.7 fusion.3
  302.8 4.4 %all_to_all.44 = f32[2,64,1,128]{3,1,2,0:T(8,128)S(1)} all-to-all(f32[2,64,1,128]{3,1,2,0:T(8,128)S(1)} %bitcast.102), channel_id=1, replica_groups=mesh['band_0'=4,'band_1'=4,'band_2'=4,'band_3'=2] {'band_3'}, dimensions={0} | all-to-all | bytes 131072 | tf_op jit(solution)/shard_map/all_to_all | solution.py:29
  307.2 12.8 %all_to_all.45 = f32[64,1,128]{2,1,0:T(1,128)S(1)} all-to-all(f32[64,1,128]{2,1,0:T(1,128)S(1)} %bitcast.103), channel_id=1, replica_groups=mesh['band_0'=4,'band_1'=4,'band_2'=4,'band_3'=2] {'band_0','band_1','ba..., dimensions={0} | all-to-all | bytes 65536 | tf_op jit(solution)/shard_map/all_to_all | solution.py:37
  (209 shorter events, 95.5 us)
Async XLA Ops:
  0.6 18.4 %copy-start.4 = (f32[32]{0:T(128)S(1)}, f32[32]{0:T(128)}, u32[]{:S(2)}) copy-start(f32[32]{0:T(128)} %param.6) | copy-start | bytes 388
  0.6 133.0 %collective-permute-start.2 = (f32[1,64,4096]{2,1,0:T(8,128)}, f32[1,64,4096]{2,1,0:T(8,128)S(1)}, u32[]{:S(2)}, u32[]{:S(2)}) collective-permute-start(f32[1,64,4096]{2,1,0:T(8,128)} %param.5), channel_id=1, source_target_pairs={{0,2},{1,3},{2,4},{3,5},{4,6},{5,7},{6,8},{7,9},{8,10},{9,11},{10,... | collective-permute-start | bytes 3145736 | tf_op jit(solution)/shard_map/ppermute | solution.py:19
  2.7 172.8 %collective-permute-start = (f32[1,64,4096]{2,1,0:T(8,128)}, f32[1,64,4096]{2,1,0:T(8,128)}, u32[]{:S(2)}, u32[]{:S(2)}) collective-permute-start(f32[1,64,4096]{2,1,0:T(8,128)} %param.5), channel_id=1, source_target_pairs={{0,1},{1,2},{2,3},{3,4},{4,5},{5,6},{6,7},{7,8},{8,9},{9,10},{10,1... | collective-permute-start | bytes 3145736 | tf_op jit(solution)/shard_map/ppermute | solution.py:19
  8.3 114.9 %copy-start = (f32[1,64,4096]{2,1,0:T(8,128)S(1)}, f32[1,64,4096]{2,1,0:T(8,128)}, u32[]{:S(2)}) copy-start(f32[1,64,4096]{2,1,0:T(8,128)} %param.5) | copy-start | bytes 3145732
  8.3 263.6 %all-to-all-start.1 = ((f32[1,128,2048]{2,0,1:T(1,128)}), f32[1,128,2048]{2,0,1:T(1,128)}, u32[]{:S(2)}, u32[]{:S(2)}) async-start(f32[1,128,2048]{2,0,1:T(1,128)} %all_to_all.33), calls=%async_computation.1 | async-start | bytes 2097152 | tf_op jit(solution)/shard_map/all_to_all | solution.py:101
  122.3 77.3 %copy-start.1 = (f32[64,4096]{1,0:T(8,128)}, f32[64,4096]{1,0:T(8,128)S(1)}, u32[]{:S(2)}) copy-start(f32[64,4096]{1,0:T(8,128)S(1)} %get-tuple-element.24) | copy-start | bytes 3145732
  133.7 4.6 %copy-start.3 = (f32[1,64,4096]{2,1,0:T(8,128)}, f32[1,64,4096]{2,1,0:T(8,128)S(1)}, u32[]{:S(2)}) copy-start(f32[1,64,4096]{2,1,0:T(8,128)S(1)} %collective-permute-done.2) | copy-start | bytes 3145732
  220.9 9.6 %copy-start.2 = (f32[64,64,64]{2,1,0:T(8,128)S(1)}, f32[64,64,64]{2,1,0:T(8,128)}, u32[]{:S(2)}) copy-start(f32[64,64,64]{2,1,0:T(8,128)} %reshape.1032) | copy-start | bytes 3145732
  222.5 43.0 %collective-permute-start.1 = (f32[1,64,4096]{2,1,0:T(8,128)}, f32[1,64,4096]{2,1,0:T(8,128)}, u32[]{:S(2)}, u32[]{:S(2)}) collective-permute-start(f32[1,64,4096]{2,1,0:T(8,128)} %get-tuple-element.33), channel_id=1, source_target_pairs={{0,127},{1,0},{2,1},{3,2},{4,3},{5,4},{6,5},{7,6},{8,7},{9,8},{10,... | collective-permute-start | bytes 3145736 | tf_op jit(solution)/shard_map/ppermute | solution.py:19
  223.4 42.0 %collective-permute-start.3 = (f32[1,64,4096]{2,1,0:T(8,128)}, f32[1,64,4096]{2,1,0:T(8,128)}, u32[]{:S(2)}, u32[]{:S(2)}) collective-permute-start(f32[1,64,4096]{2,1,0:T(8,128)} %get-tuple-element.34), channel_id=1, source_target_pairs={{0,126},{1,127},{2,0},{3,1},{4,2},{5,3},{6,4},{7,5},{8,6},{9,7},{1... | collective-permute-start | bytes 3145736 | tf_op jit(solution)/shard_map/ppermute | solution.py:19
where the time goes:
time: 326 us; the launch traced here: 321 us
  local copies, waits for them, and re-layouts  152 us (47%)
  matrix products  90.8 us (28%)
  blocking collectives  45.3 us (14%)
  starting transfers between devices  22.9 us (7%)
  other arithmetic  6.92 us (2%)
    dynamic_slice x64, local copies, waits for them, and re-layouts, lookup(): return lax.map(one_plane, shell_index)  59 us
    dot_general x6, matrix products, transform(): second_pass = jnp.einsum('by,myz->mbz', table, planes, precision=highest)  36.6 us
    all_to_all x1, blocking collectives, local(): lax.all_to_all(flat_terms, BAND, split_axis=1, concat_axis=0, tiled=True)  28.1 us
    dynamic_update_slice x64, local copies, waits for them, and re-layouts, lookup(): return lax.map(one_plane, shell_index)  25.1 us
    dot_general x64, matrix products, one_plane(): jnp.dot(onehot, kernel_values, precision=highest, preferred_element_type=...  17.2 us
    dot_general x6, matrix products, transform(): first_pass = jnp.einsum('ax,nxw->naw', table, fields, precision=highest)  17.2 us
    dot_general x6, matrix products, transform(): jnp.dot(lanes, wide_table, precision=highest, preferred_element_type=jnp....  17 us
    div x6, local copies, waits for them, and re-layouts, potentials(): fields = transform(spectrum, table, wide_table) / float(extent ** 3)  16.1 us
  transfers between devices with their start and end apart: 5, of which 0 were waited for; matrix products, arithmetic and copies ran while one was open for 75% of the time, Pallas kernels for 0%

commit v1 on v0

v1 whole, which is shorter than its diff:
```python
import math

import jax
import jax.numpy as jnp
import numpy as np
from jax import lax
from jax.experimental import pallas as pl
from jax.experimental.pallas import tpu as pltpu
from jax.sharding import PartitionSpec as P

GRID = 64
WIDE = GRID * GRID
BANDS = 128
TILES = 16
TILED = (8, 32, 8, 128)
MESH = pl.DeviceIdType.MESH
f32 = jnp.float32
bf16 = jnp.bfloat16


def cas(angle):
    return math.cos(angle) + math.sin(angle)


def cas_table():
    index = np.arange(GRID)
    angle = 2.0 * math.pi / GRID * (index[:, None] * index[None] % GRID)
    return np.cos(angle) + np.sin(angle)


def frequencies(k):
    return (0, 32, 16, 48) if k == 0 else (k, 32 - k, 64 - k, 32 + k)


def mixing(k):
    table = np.zeros((4, 4))
    for t, b in enumerate(frequencies(k)):
        for q in range(4):
            part, r = q // 2, q % 2
            angle = 2.0 * math.pi * b * r / GRID
            if k == 0:
                table[q, t] = cas(angle) if (part == 0) == (b % 32 == 0) else 0.0
            elif part == 0:
                table[q, t] = cas(angle)
            else:
                sign = 1.0 if b in (k, 32 + k) else -1.0
                table[q, t] = sign * (math.sin(angle) - math.cos(angle))
    return table


def constants():
    table = cas_table()
    high = table.astype(np.float32).astype(bf16)
    low = (table - high.astype(np.float64)).astype(np.float32).astype(bf16)
    left = np.concatenate([high, low, high], axis=1)
    four = np.tile(table, (1, 4)).astype(np.float32)
    mixes = np.stack([mixing(k) for k in range(TILES)])
    forward = np.repeat(mixes.reshape(TILES * 4, 4), GRID, axis=1).astype(np.float32)
    backward = np.repeat(
        np.swapaxes(mixes, 1, 2).reshape(TILES * 4, 4), GRID, axis=1
    ).astype(np.float32)
    return left, four, forward, backward


def half_spectrum(xs):
    n = len(xs)
    if n == 2:
        return [xs[0] + xs[1], xs[0] - xs[1]], [None, None]
    even_re, even_im = half_spectrum(xs[0::2])
    odd_re, odd_im = half_spectrum(xs[1::2])
    h, q = n // 2, n // 4
    re, im = [None] * (h + 1), [None] * (h + 1)
    re[0], re[h] = even_re[0] + odd_re[0], even_re[0] - odd_re[0]
    for k in range(1, q):
        c, s = math.cos(2 * math.pi * k / n), -math.sin(2 * math.pi * k / n)
        if 2 * k == q:
            t_re, t_im = (odd_re[k] + odd_im[k]) * c, (odd_im[k] - odd_re[k]) * c
        else:
            t_re = odd_re[k] * c - odd_im[k] * s
            t_im = odd_re[k] * s + odd_im[k] * c
        re[k], im[k] = even_re[k] + t_re, even_im[k] + t_im
        re[h - k], im[h - k] = even_re[k] - t_re, t_im - even_im[k]
    re[q], im[q] = even_re[q], -odd_re[q]
    return re, im


def half_spectrum_transposed(re, im):
    h = len(re) - 1
    n = 2 * h
    if n == 2:
        return [re[0] + re[1], re[0] - re[1]]
    q = n // 4
    even_re, even_im = [None] * (q + 1), [None] * (q + 1)
    odd_re, odd_im = [None] * (q + 1), [None] * (q + 1)
    even_re[0], odd_re[0] = re[0] + re[h], re[0] - re[h]
    for k in range(1, q):
        even_re[k], even_im[k] = re[k] + re[h - k], im[k] - im[h - k]
        d_re, d_im = re[k] - re[h - k], im[k] + im[h - k]
        c, s = math.cos(2 * math.pi * k / n), math.sin(2 * math.pi * k / n)
        if 2 * k == q:
            odd_re[k], odd_im[k] = (d_re - d_im) * c, (d_re + d_im) * c
        else:
            odd_re[k], odd_im[k] = d_re * c - d_im * s, d_re * s + d_im * c
    even_re[q], odd_re[q] = re[q], -im[q]
    out = [None] * n
    out[0::2] = half_spectrum_transposed(even_re, even_im)
    out[1::2] = half_spectrum_transposed(odd_re, odd_im)
    return out


def split(x):
    high = x.astype(bf16)
    return high, (x - high.astype(f32)).astype(bf16)


def dot(a, b):
    return jnp.dot(a, b, preferred_element_type=f32)


def dot_t(a, b):
    return lax.dot_general(a, b, (((1,), (1,)), ((), ())), preferred_element_type=f32)


def lanes(index, size):
    return pl.ds(pl.multiple_of(index * size, size), size)


def remote(src, dst, send, recv, device):
    return pltpu.make_async_remote_copy(
        src_ref=src, dst_ref=dst, send_sem=send, recv_sem=recv,
        device_id=(device,), device_id_type=MESH,
    )


def read(ref, lead, m):
    pieces = [ref[*lead, :, 2 * m + i].reshape(GRID, 128) for i in range(2)]
    return jnp.concatenate(pieces, axis=1)


def kernel(
    orb, kv, shell, left, four, forward, backward, exch, margin,
    fields, work, total, screen, classes, w_high, w_low, v_high, v_low,
    grid_orb, grid_term, gram, rows,
    load_sem, send_sem, recv_sem, many_send, many_recv, out_sem,
):
    me = lax.axis_index("band")
    core = lax.rem(me, 2)
    x = lax.rem(me // 2, 4)
    plane = me // 8
    partner = me + 1 - 2 * core
    first = lax.rem(me + BANDS - 2 + 4 * core, BANDS)
    second = lax.rem(me + 2 - 4 * core + BANDS, BANDS)

    def wrap4(v):
        return lax.rem(v + 4, 4)

    load = pltpu.make_async_copy(orb, fields.at[0], load_sem.at[0])
    load.start()
    load_classes = pltpu.make_async_copy(shell, classes, load_sem.at[1])
    load_classes.start()
    load.wait()

    to_first = remote(fields.at[0], fields.at[2], send_sem.at[0], recv_sem.at[2], first)
    to_partner = remote(fields.at[0], fields.at[1], send_sem.at[1], recv_sem.at[1], partner)
    to_second = remote(fields.at[0], fields.at[4], send_sem.at[2], recv_sem.at[4], second)
    forward_on = remote(fields.at[2], fields.at[3], send_sem.at[3], recv_sem.at[3], partner)
    to_first.start()
    to_partner.start()

    def send_slice(slot, orbital, owner):
        remote(
            fields.at[slot, lax.rem(owner, 8), pl.ds(owner // 8 * 2, 2)],
            grid_orb.at[pl.ds(orbital * 2, 2)],
            many_send.at[0], many_recv.at[0], owner,
        ).start()

    def send_near(slot, orbital):
        def one(t, carry):
            there = lax.rem(plane + t // 2, 16)
            side = lax.rem(core + t, 2)
            send_slice(slot, orbital, there * 8 + x * 2 + side)
            return carry

        lax.fori_loop(1, 32, one, 0)
        grid_orb[pl.ds(orbital * 2, 2)] = fields[slot, lax.rem(me, 8), pl.ds(plane * 2, 2)]

    def send_across(slot, orbital, x_there, side):
        def one(t, carry):
            there = lax.rem(plane + t, 16)
            send_slice(slot, orbital, there * 8 + x_there * 2 + side)
            return carry

        lax.fori_loop(0, 16, one, 0)

    send_near(0, me)

    def make_tables(k, carry):
        for q in range(4):
            rows_here = pl.ds(q * GRID, GRID)
            high, low = split(four[...] * forward[pl.ds(k * 4 + q, 1), :])
            w_high[k, rows_here, :] = high
            w_low[k, rows_here, :] = low
            high, low = split(four[...] * backward[pl.ds(k * 4 + q, 1), :])
            v_high[k, rows_here, :] = high
            v_low[k, rows_here, :] = low
        return carry

    lax.fori_loop(0, TILES, make_tables, 0)

    load_classes.wait()
    values = [kv[i] * (-1.0 / GRID**3) for i in range(32)]

    def look_up(index):
        level = values
        bit = 1
        while len(level) > 1:
            picked = (index & bit) != 0
            level = [
                jnp.where(picked, level[i + 1], level[i]) for i in range(0, len(level), 2)
            ]
            bit *= 2
        return level[0]

    def make_screen(g, carry):
        here = lanes(g, 8)
        left_half = lax.broadcasted_iota(jnp.int32, (8, 128), 1) < GRID

        def chunk(i):
            return classes[here, pl.ds(i * 128, 128)]

        def turned(i):
            return pltpu.roll(chunk(i), GRID, 1)

        for k in range(TILES):
            if k == 0:
                pair = (
                    jnp.where(left_half, chunk(0), turned(16)),
                    jnp.where(left_half, chunk(8), turned(24)),
                )
                screen[here, pl.ds(0, 128)] = look_up(pair[0])
                screen[here, pl.ds(128, 128)] = look_up(pair[1])
                continue
            if k % 2 == 0:
                mixed = jnp.where(left_half, chunk(k // 2), turned((32 - k) // 2))
            else:
                mixed = jnp.where(left_half, turned((k - 1) // 2), chunk((31 - k) // 2))
            found = look_up(mixed)
            screen[here, pl.ds(k * 256, 128)] = found
            screen[here, pl.ds(k * 256 + 128, 128)] = found
        return carry

    lax.fori_loop(0, 8, make_screen, 0)
    total[...] = jnp.zeros_like(total)

    def left_pass(value):
        high, low = split(value)
        return dot(left[...], jnp.concatenate([high, high, low], axis=0))

    def send_terms(j):
        def one(g, carry):
            owner = j * 8 + g

            @pl.when(owner != me)
            def _():
                remote(
                    total.at[g, pl.ds(j * 2, 2)],
                    grid_term.at[pl.ds(me * 2, 2)],
                    many_send.at[1], many_recv.at[1], owner,
                ).start()

            return carry

        lax.fori_loop(0, 8, one, 0)

    def one_pair(it, carry):
        @pl.when(it == 1)
        def _():
            to_partner.wait_recv()

        @pl.when(it == 2)
        def _():
            to_first.wait_send()
            to_second.start()
            to_first.wait_recv()
            forward_on.start()
            send_near(2, second)
            send_across(2, second, wrap4(x - 1 + 2 * core), 1 - core)

        @pl.when(it == 3)
        def _():
            forward_on.wait_recv()

        @pl.when(it == 4)
        def _():
            to_second.wait_recv()
            send_near(4, first)
            send_across(4, first, wrap4(x + 1 - 2 * core), core)

        def first_stage(m, c):
            here = lanes(m, 256)
            work[:, here] = left_pass(read(fields, (0,), m) * read(fields, (it,), m))
            return c

        lax.fori_loop(0, 16, first_stage, 0)

        def second_stage(g, c):
            here = lanes(g, 8)
            re, im = half_spectrum([work[here, pl.ds(n * 128, 128)] for n in range(32)])
            work[here, pl.ds(0, 128)] = re[0]
            work[here, pl.ds(128, 128)] = re[16]
            for k in range(1, 16):
                work[here, pl.ds(k * 256, 128)] = re[k]
                work[here, pl.ds(k * 256 + 128, 128)] = im[k]
            return c

        lax.fori_loop(0, 8, second_stage, 0)

        def third_stage(k, c):
            here = lanes(k, 256)
            high, low = split(work[:, here])
            spectrum = dot(high, w_high[k]) + dot(low, w_high[k]) + dot(high, w_low[k])
            high, low = split(spectrum * screen[:, here])
            work[:, here] = dot(high, v_high[k]) + dot(low, v_high[k]) + dot(high, v_low[k])
            return c

        lax.fori_loop(0, 16, third_stage, 0)

        def fourth_stage(g, c):
            here = lanes(g, 8)
            re = [work[here, pl.ds(0, 128)]]
            im = [None]
            for k in range(1, 16):
                re.append(work[here, pl.ds(k * 256, 128)])
                im.append(work[here, pl.ds(k * 256 + 128, 128)])
            re.append(work[here, pl.ds(128, 128)])
            im.append(None)
            out = half_spectrum_transposed(re, im)
            for n in range(32):
                work[here, pl.ds(n * 128, 128)] = out[n]
            return c

        lax.fori_loop(0, 8, fourth_stage, 0)

        def fifth_stage(m, c):
            j = lax.rem(plane + m, 16)
            added = left_pass(work[:, lanes(j, 256)])
            for i in range(2):
                part = added[:, i * 128 : i * 128 + 128].reshape(8, 8, 128)
                total[:, 2 * j + i] += part * fields[it, :, 2 * j + i]

            @pl.when(jnp.logical_and(it == 4, m > 0))
            def _():
                send_terms(lax.rem(plane + m + 15, 16))

            return c

        lax.fori_loop(0, 16, fifth_stage, 0)
        return carry

    lax.fori_loop(0, 5, one_pair, 0)
    send_terms(lax.rem(plane + 15, 16))
    write = pltpu.make_async_copy(total, exch, out_sem)
    write.start()
    grid_term[pl.ds(me * 2, 2)] = total[lax.rem(me, 8), pl.ds(plane * 2, 2)]

    def wait_many(count, buffer, index):
        part = buffer.at[pl.ds(0, count)]
        remote(part, part, many_send.at[index], many_recv.at[index], partner).wait_recv()

    wait_many(125 * 2, grid_orb, 0)
    wait_many(127 * 2, grid_term, 1)
    def across(buffer, s):
        flat = buffer.reshape(BANDS * 16, 128)
        return jnp.concatenate(
            [flat[pl.ds(8 * i + s, BANDS, stride=16), :] for i in range(2)], axis=1
        )

    result = jnp.zeros((BANDS, BANDS), f32)
    for s in range(8):
        a_high, a_low = split(across(grid_orb, s))
        b_high, b_low = split(across(grid_term, s))
        result += dot_t(a_high, b_high) + dot_t(a_low, b_high) + dot_t(a_high, b_low)
    result = result * (1.0 / GRID**3)
    for i in range(BANDS):
        gram[i] = result[i : i + 1, :]

    def send_row(t, carry):
        owner = lax.rem(me + t, BANDS)
        remote(
            gram.at[owner], rows.at[me], many_send.at[2], many_recv.at[2], owner
        ).start()
        return carry

    lax.fori_loop(1, BANDS, send_row, 0)
    rows[me] = gram[me]
    part = rows.at[pl.ds(0, BANDS - 1)]
    remote(part, part, many_send.at[2], many_recv.at[2], partner).wait_recv()
    margin[...] = jnp.sum(rows[...], axis=0)

    to_partner.wait_send()
    to_second.wait_send()
    forward_on.wait_send()
    part = grid_orb.at[pl.ds(0, 125 * 2)]
    remote(part, part, many_send.at[0], many_recv.at[0], partner).wait_send()
    part = grid_term.at[pl.ds(0, 127 * 2)]
    remote(part, part, many_send.at[1], many_recv.at[1], partner).wait_send()
    part = rows.at[pl.ds(0, BANDS - 1)]
    remote(part, part, many_send.at[2], many_recv.at[2], partner).wait_send()
    write.wait()


def local(orbitals, kernel_values, shell_index):
    any_space = pl.BlockSpec(memory_space=pl.ANY)
    vmem = pl.BlockSpec(memory_space=pltpu.VMEM)
    exchange, margin = pl.pallas_call(
        kernel,
        out_shape=(
            jax.ShapeDtypeStruct(TILED, f32),
            jax.ShapeDtypeStruct((1, BANDS), f32),
        ),
        in_specs=[any_space, pl.BlockSpec(memory_space=pltpu.SMEM), any_space] + [vmem] * 4,
        out_specs=(any_space, vmem),
        scratch_shapes=[
            pltpu.VMEM((5, *TILED), f32),
            pltpu.VMEM((GRID, WIDE), f32),
            pltpu.VMEM(TILED, f32),
            pltpu.VMEM((GRID, WIDE), f32),
            pltpu.VMEM((GRID, WIDE), jnp.int32),
            pltpu.VMEM((TILES, 256, 256), bf16),
            pltpu.VMEM((TILES, 256, 256), bf16),
            pltpu.VMEM((TILES, 256, 256), bf16),
            pltpu.VMEM((TILES, 256, 256), bf16),
            pltpu.VMEM((BANDS * 2, 8, 128), f32),
            pltpu.VMEM((BANDS * 2, 8, 128), f32),
            pltpu.VMEM((BANDS, 1, BANDS), f32),
            pltpu.VMEM((BANDS, 1, BANDS), f32),
            pltpu.SemaphoreType.DMA((2,)),
            pltpu.SemaphoreType.DMA((4,)),
            pltpu.SemaphoreType.DMA((5,)),
            pltpu.SemaphoreType.DMA((3,)),
            pltpu.SemaphoreType.DMA((3,)),
            pltpu.SemaphoreType.DMA,
        ],
        compiler_params=pltpu.CompilerParams(
            has_side_effects=True, vmem_limit_bytes=56 * 1024 * 1024
        ),
        name="exchange",
    )(
        orbitals.reshape(8, 8, 32, 128).transpose(0, 2, 1, 3),
        kernel_values,
        shell_index,
        *[jnp.asarray(c) for c in constants()],
    )
    return exchange.transpose(0, 2, 1, 3).reshape(1, GRID, WIDE), margin


def solution(mesh):
    return jax.shard_map(
        local,
        mesh=mesh,
        in_specs=(P("band", None, None), P(), P()),
        out_specs=(P("band", None, None), P("band", None)),
        check_vma=False,
    )
```

time: 326 us -> 111 us (0.34); the launches traced: 321 us -> 111 us
  local copies, waits for them, and re-layouts: 152 us -> 2.79 us
  Pallas kernels: 0 us -> 108 us
  matrix products: 90.8 us -> 0 us
  blocking collectives: 45.3 us -> 0 us
  starting transfers between devices: 22.9 us -> 0 us
  other arithmetic: 6.92 us -> 0 us
    pallas_call x0 -> x1, Pallas kernels: none -> 108 us  [local(): pl.pallas_call(kernel, out_shape=(jax.ShapeDtypeStruct(TILED, f32), jax.S...]
    dot_general x83 -> x0, matrix products: 90.8 us -> none  [the longest x6 36.6 us: transform(): second_pass = jnp.einsum('by,myz->mbz', table, planes, precision=highest)]
    dynamic_slice x64 -> x0, local copies, waits for them, and re-layouts: 59 us -> none  [lookup(): return lax.map(one_plane, shell_index)]
    all_to_all x3 -> x0, blocking collectives: 45.3 us -> none  [the longest x1 28.1 us: local(): lax.all_to_all(flat_terms, BAND, split_axis=1, concat_axis=0, tiled=True)]
    reshape x15 -> x0, local copies, waits for them, and re-layouts: 36.7 us -> none  [the longest x6 14.5 us: transform(): planes = third_pass.reshape(batch_rows * extent, extent, extent)]
    dynamic_update_slice x64 -> x0, local copies, waits for them, and re-layouts: 25.1 us -> none  [lookup(): return lax.map(one_plane, shell_index)]
    div x6 -> x0, local copies, waits for them, and re-layouts: 16.1 us -> none  [potentials(): fields = transform(spectrum, table, wide_table) / float(extent ** 3)]
    ppermute x4 -> x0, starting transfers between devices: 12.2 us -> none  [from_behind(): return lax.ppermute(value, axis, pairs)]
  transfers between devices with their start and end apart: 5 -> 0, of which waited for: 0 -> 0; matrix products, arithmetic and copies ran while one was open for 75% -> 0% of each run, Pallas kernels for 0% -> 0%
where the time goes in v1:
time: 111 us
  Pallas kernels  108 us (97%)
  local copies, waits for them, and re-layouts  2.79 us (3%)
    pallas_call x1, Pallas kernels, local(): pl.pallas_call(kernel, out_shape=(jax.ShapeDtypeStruct(TILED, f32), jax.S...  108 us
    unnamed x4, local copies, waits for them, and re-layouts  2.79 us

profile of v1, /device:TPU:1, one launch (start us, length us, event | category | flops | bytes accessed | tf_op | source)
XLA Modules:
  0.0 111.2 jit_solution(7312905661457554488)
XLA Ops:
  0.6 107.7 %exchange.1 = (f32[8,32,8,128]{3,2,1,0:T(8,128)}, f32[1,128]{1,0:T(1,128)}) custom-call(f32[8,32,8,128]{3,2,1,0:T(8,128)} %bitcast.6, f32[32]{0:T(128)} %kv.1, s32[64,4096]{1,0:T(8,128)} %shell.1, bf16[64,192]{1,0:T(8,128)(2,1)} %constant.8.clone.left, f32[64,256]{1,0:T(8,128)} %constant.9.clone.four, f32[64,256]{1,0:T(8,128)} %constant.10.clone.forward, ...), custom_call_target="tpu_custom_call" | custom-call | tf_op jit(solution)/shard_map/exchange/pallas_call | solution.py:415
  108.4 0.0 copy-start
  108.4 2.3 %copy.11 = f32[1,64,4096]{2,1,0:T(8,128)} copy(f32[1,64,4096]{2,1,0:T(8,128)} %bitcast.7) | data formatting | bytes 2097152
  110.7 0.0 copy-done
  110.7 0.5 copy.12
Async XLA Ops:
  108.4 2.3 %copy-start = (f32[1,128]{1,0:T(1,128)S(1)}, f32[1,128]{1,0:T(1,128)}, u32[]{:S(2)}) copy-start(f32[1,128]{1,0:T(1,128)} %get-tuple-element.9) | copy-start | bytes 1540

commit v2 on v1

--- a/solution.py
+++ b/solution.py
@@ -301,7 +301,7 @@
             work[:, here] = left_pass(read(fields, (0,), m) * read(fields, (it,), m))
             return c
 
-        lax.fori_loop(0, 16, first_stage, 0)
+        lax.fori_loop(0, 16, first_stage, 0, unroll=True)
 
         def second_stage(g, c):
             here = lanes(g, 8)
@@ -323,7 +323,7 @@
             work[:, here] = dot(high, v_high[k]) + dot(low, v_high[k]) + dot(high, v_low[k])
             return c
 
-        lax.fori_loop(0, 16, third_stage, 0)
+        lax.fori_loop(0, 16, third_stage, 0, unroll=True)
 
         def fourth_stage(g, c):
             here = lanes(g, 8)
@@ -348,13 +348,16 @@
                 part = added[:, i * 128 : i * 128 + 128].reshape(8, 8, 128)
                 total[:, 2 * j + i] += part * fields[it, :, 2 * j + i]
 
-            @pl.when(jnp.logical_and(it == 4, m > 0))
-            def _():
-                send_terms(lax.rem(plane + m + 15, 16))
+            if m > 0:
+
+                @pl.when(it == 4)
+                def _():
+                    send_terms(lax.rem(plane + m + 15, 16))
 
             return c
 
-        lax.fori_loop(0, 16, fifth_stage, 0)
+        for m in range(16):
+            fifth_stage(m, 0)
         return carry
 
     lax.fori_loop(0, 5, one_pair, 0)

time: 111 us -> 78.6 us (0.71)
  Pallas kernels: 108 us -> 75 us
    pallas_call x1, Pallas kernels: 108 us -> 75 us  [local(): pl.pallas_call(kernel, out_shape=(jax.ShapeDtypeStruct(TILED, f32), jax.S...]
where the time goes in v2:
time: 78.6 us; the launch traced here: 78.4 us
  Pallas kernels  75 us (95%)
  local copies, waits for them, and re-layouts  2.79 us (4%)
    pallas_call x1, Pallas kernels, local(): pl.pallas_call(kernel, out_shape=(jax.ShapeDtypeStruct(TILED, f32), jax.S...  75 us
    unnamed x4, local copies, waits for them, and re-layouts  2.79 us

profile of v2, /device:TPU:1, one launch (start us, length us, event | category | flops | bytes accessed | tf_op | source)
XLA Modules:
  0.0 78.4 jit_solution(3638592804015663818)
XLA Ops:
  0.6 75.0 %exchange.1 = (f32[8,32,8,128]{3,2,1,0:T(8,128)}, f32[1,128]{1,0:T(1,128)}) custom-call(f32[8,32,8,128]{3,2,1,0:T(8,128)} %bitcast.6, f32[32]{0:T(128)} %kv.1, s32[64,4096]{1,0:T(8,128)} %shell.1, bf16[64,192]{1,0:T(8,128)(2,1)} %constant.8.clone.left, f32[64,256]{1,0:T(8,128)} %constant.9.clone.four, f32[64,256]{1,0:T(8,128)} %constant.10.clone.forward, ...), custom_call_target="tpu_custom_call" | custom-call | tf_op jit(solution)/shard_map/exchange/pallas_call | solution.py:418
  75.6 0.0 copy-start
  75.6 2.3 %copy.11 = f32[1,64,4096]{2,1,0:T(8,128)} copy(f32[1,64,4096]{2,1,0:T(8,128)} %bitcast.7) | data formatting | bytes 2097152
  77.9 0.0 copy-done
  77.9 0.5 copy.12
Async XLA Ops:
  75.6 2.3 %copy-start = (f32[1,128]{1,0:T(1,128)S(1)}, f32[1,128]{1,0:T(1,128)}, u32[]{:S(2)}) copy-start(f32[1,128]{1,0:T(1,128)} %get-tuple-element.9) | copy-start | bytes 1540

commit v3 on v2

--- a/solution.py
+++ b/solution.py
@@ -13,6 +13,10 @@
 BANDS = 128
 TILES = 16
 TILED = (8, 32, 8, 128)
+SHIFTS = sorted(
+    ((dz, dy) for dz in range(4) for dy in range(4)),
+    key=lambda s: -min(s[0], 4 - s[0]) - min(s[1], 4 - s[1]),
+)
 MESH = pl.DeviceIdType.MESH
 f32 = jnp.float32
 bf16 = jnp.bfloat16
@@ -138,10 +142,10 @@
 
 
 def kernel(
-    orb, kv, shell, left, four, forward, backward, exch, margin,
-    fields, work, total, screen, classes, w_high, w_low, v_high, v_low,
-    grid_orb, grid_term, gram, rows,
-    load_sem, send_sem, recv_sem, many_send, many_recv, out_sem,
+    orb, kv, shell, left_in, four_in, forward_in, backward_in, total, margin,
+    fields, work, screen, classes, left, four, forward, backward,
+    w_high, w_low, v_high, v_low, grid_orb, grid_term, gram, rows,
+    load_sem, send_sem, recv_sem, part_send, part_recv, many_send, many_recv, meet_sem,
 ):
     me = lax.axis_index("band")
     core = lax.rem(me, 2)
@@ -154,17 +158,53 @@
     def wrap4(v):
         return lax.rem(v + 4, 4)
 
+    def plane_at(dz, dy):
+        return wrap4(plane // 4 + dz) * 4 + wrap4(plane + dy)
+
     load = pltpu.make_async_copy(orb, fields.at[0], load_sem.at[0])
     load.start()
-    load_classes = pltpu.make_async_copy(shell, classes, load_sem.at[1])
-    load_classes.start()
+
+    meetings = [partner]
+    neighbours = [first, second]
+    for scale in (2, 8, 32):
+        here = lax.rem(me // scale, 4)
+        base = me - here * scale
+        meetings.append(me + scale * (1 - 2 * lax.rem(here, 2)))
+        meetings.append(base + scale * (3 - here))
+    barrier = pltpu.get_barrier_semaphore()
+    for device in neighbours + meetings:
+        pl.semaphore_signal(barrier, inc=1, device_id=(device,), device_id_type=MESH)
+    small = [
+        pltpu.make_async_copy(src, dst, load_sem.at[i + 1])
+        for i, (src, dst) in enumerate(
+            [(four_in, four), (forward_in, forward), (backward_in, backward),
+             (left_in, left), (shell, classes)]
+        )
+    ]
+    for copy in small:
+        copy.start()
+    pl.semaphore_wait(barrier, len(neighbours + meetings))
     load.wait()
 
-    to_first = remote(fields.at[0], fields.at[2], send_sem.at[0], recv_sem.at[2], first)
-    to_partner = remote(fields.at[0], fields.at[1], send_sem.at[1], recv_sem.at[1], partner)
-    to_second = remote(fields.at[0], fields.at[4], send_sem.at[2], recv_sem.at[4], second)
-    forward_on = remote(fields.at[2], fields.at[3], send_sem.at[3], recv_sem.at[3], partner)
-    to_first.start()
+    to_partner = remote(fields.at[0], fields.at[1], send_sem.at[0], recv_sem.at[0], partner)
+    forward_on = remote(fields.at[2], fields.at[3], send_sem.at[1], recv_sem.at[1], partner)
+
+    def send_field(slot, part, device, below):
+        start = 2 * lax.rem(device // 2, 4) - below + 8
+        for i in range(8):
+            group = lax.rem(start + i, 8)
+            index = part if i < 3 else part + 1
+            remote(
+                fields.at[0, group], fields.at[slot, group],
+                part_send.at[index], part_recv.at[index], device,
+            ).start()
+
+    def wait_field(slot, part):
+        count = 3 if part % 2 == 0 else 5
+        ref = fields.at[slot, pl.ds(0, count)]
+        return remote(ref, ref, part_send.at[part], part_recv.at[part], partner)
+
+    send_field(2, 0, first, 1 - core)
     to_partner.start()
 
     def send_slice(slot, orbital, owner):
@@ -191,8 +231,6 @@
             return carry
 
         lax.fori_loop(0, 16, one, 0)
-
-    send_near(0, me)
 
     def make_tables(k, carry):
         for q in range(4):
@@ -205,9 +243,19 @@
             v_low[k, rows_here, :] = low
         return carry
 
-    lax.fori_loop(0, TILES, make_tables, 0)
-
-    load_classes.wait()
+    for copy in small[:3]:
+        copy.wait()
+    for step, device in enumerate(meetings):
+        pl.semaphore_signal(
+            meet_sem.at[step], inc=1, device_id=(device,), device_id_type=MESH
+        )
+        lax.fori_loop(2 * step, 2 * step + 2, make_tables, 0)
+        pl.semaphore_wait(meet_sem.at[step], 1)
+    send_near(0, me)
+    lax.fori_loop(14, TILES, make_tables, 0)
+
+    for copy in small[3:]:
+        copy.wait()
     values = [kv[i] * (-1.0 / GRID**3) for i in range(32)]
 
     def look_up(index):
@@ -279,12 +327,14 @@
 
         @pl.when(it == 2)
         def _():
-            to_first.wait_send()
-            to_second.start()
-            to_first.wait_recv()
-            forward_on.start()
+            for part in range(2):
+                wait_field(2, part).wait_send()
+            send_field(4, 2, second, core)
+            wait_field(2, 0).wait_recv()
             send_near(2, second)
             send_across(2, second, wrap4(x - 1 + 2 * core), 1 - core)
+            wait_field(2, 1).wait_recv()
+            forward_on.start()
 
         @pl.when(it == 3)
         def _():
@@ -292,9 +342,10 @@
 
         @pl.when(it == 4)
         def _():
-            to_second.wait_recv()
+            wait_field(4, 2).wait_recv()
             send_near(4, first)
             send_across(4, first, wrap4(x + 1 - 2 * core), core)
+            wait_field(4, 3).wait_recv()
 
         def first_stage(m, c):
             here = lanes(m, 256)
@@ -341,29 +392,22 @@
 
         lax.fori_loop(0, 8, fourth_stage, 0)
 
-        def fifth_stage(m, c):
-            j = lax.rem(plane + m, 16)
+        for m, (dz, dy) in enumerate(SHIFTS):
+            j = plane_at(dz, dy)
             added = left_pass(work[:, lanes(j, 256)])
             for i in range(2):
                 part = added[:, i * 128 : i * 128 + 128].reshape(8, 8, 128)
                 total[:, 2 * j + i] += part * fields[it, :, 2 * j + i]
-
             if m > 0:
 
                 @pl.when(it == 4)
                 def _():
-                    send_terms(lax.rem(plane + m + 15, 16))
-
-            return c
-
-        for m in range(16):
-            fifth_stage(m, 0)
+                    send_terms(plane_at(*SHIFTS[m - 1]))
+
         return carry
 
     lax.fori_loop(0, 5, one_pair, 0)
-    send_terms(lax.rem(plane + 15, 16))
-    write = pltpu.make_async_copy(total, exch, out_sem)
-    write.start()
+    send_terms(plane)
     grid_term[pl.ds(me * 2, 2)] = total[lax.rem(me, 8), pl.ds(plane * 2, 2)]
 
     def wait_many(count, buffer, index):
@@ -401,58 +445,77 @@
     margin[...] = jnp.sum(rows[...], axis=0)
 
     to_partner.wait_send()
-    to_second.wait_send()
     forward_on.wait_send()
+    for part in range(2, 4):
+        wait_field(4, part).wait_send()
     part = grid_orb.at[pl.ds(0, 125 * 2)]
     remote(part, part, many_send.at[0], many_recv.at[0], partner).wait_send()
     part = grid_term.at[pl.ds(0, 127 * 2)]
     remote(part, part, many_send.at[1], many_recv.at[1], partner).wait_send()
     part = rows.at[pl.ds(0, BANDS - 1)]
     remote(part, part, many_send.at[2], many_recv.at[2], partner).wait_send()
-    write.wait()
+
+
+def finish(total, margin, exch, out, sem):
+    copy = pltpu.make_async_copy(total, exch, sem)
+    copy.start()
+    out[...] = margin[...]
+    copy.wait()
 
 
 def local(orbitals, kernel_values, shell_index):
     any_space = pl.BlockSpec(memory_space=pl.ANY)
+    hbm = pl.BlockSpec(memory_space=pltpu.HBM)
     vmem = pl.BlockSpec(memory_space=pltpu.VMEM)
-    exchange, margin = pl.pallas_call(
+    tables = constants()
+    total, margin = pl.pallas_call(
         kernel,
-        out_shape=(
-            jax.ShapeDtypeStruct(TILED, f32),
-            jax.ShapeDtypeStruct((1, BANDS), f32),
-        ),
-        in_specs=[any_space, pl.BlockSpec(memory_space=pltpu.SMEM), any_space] + [vmem] * 4,
-        out_specs=(any_space, vmem),
+        out_shape=(pltpu.VMEM(TILED, f32), pltpu.VMEM((1, BANDS), f32)),
+        in_specs=[hbm, pl.BlockSpec(memory_space=pltpu.SMEM)] + [hbm] * 5,
+        out_specs=(vmem, vmem),
         scratch_shapes=[
             pltpu.VMEM((5, *TILED), f32),
             pltpu.VMEM((GRID, WIDE), f32),
-            pltpu.VMEM(TILED, f32),
             pltpu.VMEM((GRID, WIDE), f32),
             pltpu.VMEM((GRID, WIDE), jnp.int32),
-            pltpu.VMEM((TILES, 256, 256), bf16),
-            pltpu.VMEM((TILES, 256, 256), bf16),
-            pltpu.VMEM((TILES, 256, 256), bf16),
-            pltpu.VMEM((TILES, 256, 256), bf16),
+            *[pltpu.VMEM(t.shape, t.dtype) for t in tables],
+            *[pltpu.VMEM((TILES, 256, 256), bf16)] * 4,
             pltpu.VMEM((BANDS * 2, 8, 128), f32),
             pltpu.VMEM((BANDS * 2, 8, 128), f32),
             pltpu.VMEM((BANDS, 1, BANDS), f32),
             pltpu.VMEM((BANDS, 1, BANDS), f32),
+            pltpu.SemaphoreType.DMA((6,)),
+            pltpu.SemaphoreType.DMA((2,)),
             pltpu.SemaphoreType.DMA((2,)),
             pltpu.SemaphoreType.DMA((4,)),
-            pltpu.SemaphoreType.DMA((5,)),
+            pltpu.SemaphoreType.DMA((4,)),
             pltpu.SemaphoreType.DMA((3,)),
             pltpu.SemaphoreType.DMA((3,)),
-            pltpu.SemaphoreType.DMA,
+            pltpu.SemaphoreType.REGULAR((7,)),
         ],
         compiler_params=pltpu.CompilerParams(
-            has_side_effects=True, vmem_limit_bytes=56 * 1024 * 1024
+            collective_id=0, has_side_effects=True, vmem_limit_bytes=62 * 1024 * 1024 + 768 * 1024
         ),
         name="exchange",
     )(
         orbitals.reshape(8, 8, 32, 128).transpose(0, 2, 1, 3),
         kernel_values,
         shell_index,
-        *[jnp.asarray(c) for c in constants()],
+        *[jnp.asarray(c) for c in tables],
+    )
+    exchange, margin = pl.pallas_call(
+        finish,
+        out_shape=(
+            jax.ShapeDtypeStruct(TILED, f32),
+            jax.ShapeDtypeStruct((1, BANDS), f32),
+        ),
+        in_specs=[vmem, vmem],
+        out_specs=(any_space, vmem),
+        scratch_shapes=[pltpu.SemaphoreType.DMA],
+        name="finish",
+    )(
+        pltpu.with_memory_space_constraint(total, pltpu.VMEM),
+        pltpu.with_memory_space_constraint(margin, pltpu.VMEM),
     )
     return exchange.transpose(0, 2, 1, 3).reshape(1, GRID, WIDE), margin
 

time: 78.6 us -> 71 us (0.903)
  Pallas kernels: 75 us -> 70.3 us
  local copies, waits for them, and re-layouts: 2.79 us -> 0 us
    pallas_call x1 -> x2, Pallas kernels: 75 us -> 70.3 us  [the longest x1 68.8 us: local(): pl.pallas_call(kernel, out_shape=(pltpu.VMEM(TILED, f32), pltpu.VMEM((1,...]
    unnamed x4 -> x0, local copies, waits for them, and re-layouts: 2.79 us -> none
where the time goes in v3:
time: 71 us; the launch traced here: 70.9 us
  Pallas kernels  70.3 us (99%)
    pallas_call x1, Pallas kernels, local(): pl.pallas_call(kernel, out_shape=(pltpu.VMEM(TILED, f32), pltpu.VMEM((1,...  68.8 us
    pallas_call x1, Pallas kernels, local(): pl.pallas_call(finish, out_shape=(jax.ShapeDtypeStruct(TILED, f32), jax.S...  1.49 us

profile of v3, /device:TPU:1, one launch (start us, length us, event | category | flops | bytes accessed | tf_op | source)
XLA Modules:
  0.0 70.9 jit_solution(3937273187930949307)
XLA Ops:
  0.6 68.8 %exchange.1 = (f32[8,32,8,128]{3,2,1,0:T(8,128)S(1)}, f32[1,128]{1,0:T(1,128)S(1)}) custom-call(f32[8,32,8,128]{3,2,1,0:T(8,128)} %bitcast.6, f32[32]{0:T(128)} %kv.1, s32[64,4096]{1,0:T(8,128)} %shell.1, bf16[64,192]{1,0:T(8,128)(2,1)} %constant.8.clone.left_in, f32[64,256]{1,0:T(8,128)} %constant.9.clone.four_in, f32[64,256]{1,0:T(8,128)} %constant.10.clone.forward_in, ...), custom_call_target="tpu_custom_call" | custom-call | tf_op jit(solution)/shard_map/exchange/pallas_call | solution.py:471
  69.4 1.5 %finish.1 = (f32[8,32,8,128]{3,2,1,0:T(8,128)}, f32[1,128]{1,0:T(1,128)}) custom-call(f32[8,32,8,128]{3,2,1,0:T(8,128)S(1)} %get-tuple-element.6.total, f32[1,128]{1,0:T(1,128)S(1)} %get-tuple-element.7.margin), custom_call_target="tpu_custom_call" | custom-call | tf_op jit(solution)/shard_map/finish/pallas_call | solution.py:506

commit v4 on v3

--- a/solution.py
+++ b/solution.py
@@ -12,6 +12,8 @@
 WIDE = GRID * GRID
 BANDS = 128
 TILES = 16
+SENT_TOGETHER = 4
+RELAYED = 2
 TILED = (8, 32, 8, 128)
 SHIFTS = sorted(
     ((dz, dy) for dz in range(4) for dy in range(4)),
@@ -125,6 +127,10 @@
     return lax.dot_general(a, b, (((1,), (1,)), ((), ())), preferred_element_type=f32)
 
 
+def nothing():
+    pass
+
+
 def lanes(index, size):
     return pl.ds(pl.multiple_of(index * size, size), size)
 
@@ -144,8 +150,9 @@
 def kernel(
     orb, kv, shell, left_in, four_in, forward_in, backward_in, total, margin,
     fields, work, screen, classes, left, four, forward, backward,
-    w_high, w_low, v_high, v_low, grid_orb, grid_term, gram, rows,
+    w_high, w_low, v_high, v_low, grid_orb, grid_term, gram, rows, relay,
     load_sem, send_sem, recv_sem, part_send, part_recv, many_send, many_recv, meet_sem,
+    relay_send, relay_recv,
 ):
     me = lax.axis_index("band")
     core = lax.rem(me, 2)
@@ -165,7 +172,9 @@
     load.start()
 
     meetings = [partner]
-    neighbours = [first, second]
+    neighbours = [first, second] + [
+        lax.rem(me + offset, BANDS) for offset in (6, 8, BANDS - 8, BANDS - 6)
+    ]
     for scale in (2, 8, 32):
         here = lax.rem(me // scale, 4)
         base = me - here * scale
@@ -189,9 +198,10 @@
     to_partner = remote(fields.at[0], fields.at[1], send_sem.at[0], recv_sem.at[0], partner)
     forward_on = remote(fields.at[2], fields.at[3], send_sem.at[1], recv_sem.at[1], partner)
 
-    def send_field(slot, part, device, below):
+    def send_field(slot, part, phase, device, below, crosses, relay_device):
         start = 2 * lax.rem(device // 2, 4) - below + 8
-        for i in range(8):
+
+        def direct(i):
             group = lax.rem(start + i, 8)
             index = part if i < 3 else part + 1
             remote(
@@ -199,12 +209,61 @@
                 part_send.at[index], part_recv.at[index], device,
             ).start()
 
+        @pl.when(crosses)
+        def _():
+            for i in range(RELAYED):
+                remote(
+                    fields.at[0, lax.rem(start + 8 - RELAYED + i, 8)],
+                    relay.at[phase, i],
+                    part_send.at[part + 1], relay_recv.at[phase], relay_device,
+                ).start()
+
+        for i in range(8 - RELAYED):
+            direct(i)
+
+        @pl.when(jnp.logical_not(crosses))
+        def _():
+            for i in range(8 - RELAYED, 8):
+                direct(i)
+
+    def pass_on(slot, part, phase, crosses):
+        @pl.when(crosses)
+        def _():
+            up = x // 3
+            device = lax.rem(me + 6 - 12 * up + BANDS, BANDS)
+            below = (1 - core) if phase == 0 else core
+            start = 2 * (3 - 3 * up) - below + 8
+            for i in range(RELAYED):
+                ref = relay.at[phase, pl.ds(0, RELAYED)]
+                if i == 0:
+                    remote(
+                        ref, ref, relay_send.at[phase], relay_recv.at[phase], partner
+                    ).wait_recv()
+                remote(
+                    relay.at[phase, i],
+                    fields.at[slot, lax.rem(start + 8 - RELAYED + i, 8)],
+                    relay_send.at[phase], part_recv.at[part + 1], device,
+                ).start()
+
+    def passed_on(phase, crosses):
+        @pl.when(crosses)
+        def _():
+            ref = relay.at[phase, pl.ds(0, RELAYED)]
+            remote(
+                ref, ref, relay_send.at[phase], relay_recv.at[phase], partner
+            ).wait_send()
+
     def wait_field(slot, part):
         count = 3 if part % 2 == 0 else 5
         ref = fields.at[slot, pl.ds(0, count)]
         return remote(ref, ref, part_send.at[part], part_recv.at[part], partner)
 
-    send_field(2, 0, first, 1 - core)
+    first_crosses = x == 3 * core
+    second_crosses = x == 3 - 3 * core
+    send_field(
+        2, 0, 0, first, 1 - core, first_crosses,
+        lax.rem(me - 8 + 16 * core + BANDS, BANDS),
+    )
     to_partner.start()
 
     def send_slice(slot, orbital, owner):
@@ -231,6 +290,14 @@
             return carry
 
         lax.fori_loop(0, 16, one, 0)
+
+    def meet(step):
+        pl.semaphore_signal(
+            meet_sem.at[step], inc=1, device_id=(meetings[step],), device_id_type=MESH
+        )
+
+    def met(step):
+        pl.semaphore_wait(meet_sem.at[step], 1)
 
     def make_tables(k, carry):
         for q in range(4):
@@ -245,14 +312,9 @@
 
     for copy in small[:3]:
         copy.wait()
-    for step, device in enumerate(meetings):
-        pl.semaphore_signal(
-            meet_sem.at[step], inc=1, device_id=(device,), device_id_type=MESH
-        )
-        lax.fori_loop(2 * step, 2 * step + 2, make_tables, 0)
-        pl.semaphore_wait(meet_sem.at[step], 1)
-    send_near(0, me)
-    lax.fori_loop(14, TILES, make_tables, 0)
+    meet(0)
+    lax.fori_loop(0, TILES, make_tables, 0)
+    met(0)
 
     for copy in small[3:]:
         copy.wait()
@@ -297,12 +359,19 @@
             screen[here, pl.ds(k * 256 + 128, 128)] = found
         return carry
 
-    lax.fori_loop(0, 8, make_screen, 0)
-    total[...] = jnp.zeros_like(total)
+    for step in (1, 2):
+        meet(step)
+        lax.fori_loop(4 * step - 4, 4 * step, make_screen, 0)
+        met(step)
 
     def left_pass(value):
         high, low = split(value)
         return dot(left[...], jnp.concatenate([high, high, low], axis=0))
+
+    def right_pass(value, w, w_rest):
+        high, low = split(value)
+        both = dot(jnp.concatenate([high, low], axis=0), w)
+        return both[:GRID] + both[GRID:] + dot(high, w_rest)
 
     def send_terms(j):
         def one(g, carry):
@@ -320,39 +389,16 @@
 
         lax.fori_loop(0, 8, one, 0)
 
-    def one_pair(it, carry):
-        @pl.when(it == 1)
-        def _():
-            to_partner.wait_recv()
-
-        @pl.when(it == 2)
-        def _():
-            for part in range(2):
-                wait_field(2, part).wait_send()
-            send_field(4, 2, second, core)
-            wait_field(2, 0).wait_recv()
-            send_near(2, second)
-            send_across(2, second, wrap4(x - 1 + 2 * core), 1 - core)
-            wait_field(2, 1).wait_recv()
-            forward_on.start()
-
-        @pl.when(it == 3)
-        def _():
-            forward_on.wait_recv()
-
-        @pl.when(it == 4)
-        def _():
-            wait_field(4, 2).wait_recv()
-            send_near(4, first)
-            send_across(4, first, wrap4(x + 1 - 2 * core), core)
-            wait_field(4, 3).wait_recv()
-
+    def one_pair(it, after=None):
+        last = it == 4
+        after = after or {}
         def first_stage(m, c):
             here = lanes(m, 256)
             work[:, here] = left_pass(read(fields, (0,), m) * read(fields, (it,), m))
             return c
 
         lax.fori_loop(0, 16, first_stage, 0, unroll=True)
+        after.get(1, nothing)()
 
         def second_stage(g, c):
             here = lanes(g, 8)
@@ -365,16 +411,16 @@
             return c
 
         lax.fori_loop(0, 8, second_stage, 0)
+        after.get(2, nothing)()
 
         def third_stage(k, c):
             here = lanes(k, 256)
-            high, low = split(work[:, here])
-            spectrum = dot(high, w_high[k]) + dot(low, w_high[k]) + dot(high, w_low[k])
-            high, low = split(spectrum * screen[:, here])
-            work[:, here] = dot(high, v_high[k]) + dot(low, v_high[k]) + dot(high, v_low[k])
+            spectrum = right_pass(work[:, here], w_high[k], w_low[k])
+            work[:, here] = right_pass(spectrum * screen[:, here], v_high[k], v_low[k])
             return c
 
         lax.fori_loop(0, 16, third_stage, 0, unroll=True)
+        after.get(3, nothing)()
 
         def fourth_stage(g, c):
             here = lanes(g, 8)
@@ -391,23 +437,61 @@
             return c
 
         lax.fori_loop(0, 8, fourth_stage, 0)
-
-        for m, (dz, dy) in enumerate(SHIFTS):
-            j = plane_at(dz, dy)
-            added = left_pass(work[:, lanes(j, 256)])
-            for i in range(2):
-                part = added[:, i * 128 : i * 128 + 128].reshape(8, 8, 128)
-                total[:, 2 * j + i] += part * fields[it, :, 2 * j + i]
-            if m > 0:
-
-                @pl.when(it == 4)
-                def _():
-                    send_terms(plane_at(*SHIFTS[m - 1]))
-
-        return carry
-
-    lax.fori_loop(0, 5, one_pair, 0)
-    send_terms(plane)
+        after.get(4, nothing)()
+
+        for start in range(0, 16, SENT_TOGETHER):
+            for dz, dy in SHIFTS[start : start + SENT_TOGETHER]:
+                j = plane_at(dz, dy)
+                added = left_pass(work[:, lanes(j, 256)])
+                for i in range(2):
+                    part = added[:, i * 128 : i * 128 + 128].reshape(8, 8, 128)
+                    term = part * fields[it, :, 2 * j + i]
+                    if it == 0:
+                        total[:, 2 * j + i] = term
+                    else:
+                        total[:, 2 * j + i] += term
+            if last and start > 0:
+                for shift in SHIFTS[start - SENT_TOGETHER : start]:
+                    send_terms(plane_at(*shift))
+
+    def next_step(step):
+        met(step)
+        meet(step + 1)
+
+    def pass_orbital(slot, part, orbital, x_there, side):
+        wait_field(slot, part).wait_recv()
+        send_near(slot, orbital)
+        send_across(slot, orbital, x_there, side)
+
+    meet(3)
+    one_pair(
+        0,
+        {1: lambda: next_step(3), 2: lambda: next_step(4), 3: lambda: next_step(5),
+         4: lambda: met(6)},
+    )
+    pass_on(2, 0, 0, first_crosses)
+    send_near(0, me)
+    to_partner.wait_recv()
+    one_pair(
+        1, {2: lambda: pass_orbital(2, 0, second, wrap4(x - 1 + 2 * core), 1 - core)}
+    )
+    for part in range(2):
+        wait_field(2, part).wait_send()
+    send_field(
+        4, 2, 1, second, core, second_crosses, lax.rem(me + 8 - 16 * core + BANDS, BANDS)
+    )
+    wait_field(2, 1).wait_recv()
+    forward_on.start()
+    one_pair(2)
+    pass_on(4, 2, 1, second_crosses)
+    forward_on.wait_recv()
+    one_pair(
+        3, {2: lambda: pass_orbital(4, 2, first, wrap4(x + 1 - 2 * core), core)}
+    )
+    wait_field(4, 3).wait_recv()
+    one_pair(4)
+    for shift in SHIFTS[16 - SENT_TOGETHER :]:
+        send_terms(plane_at(*shift))
     grid_term[pl.ds(me * 2, 2)] = total[lax.rem(me, 8), pl.ds(plane * 2, 2)]
 
     def wait_many(count, buffer, index):
@@ -448,6 +532,8 @@
     forward_on.wait_send()
     for part in range(2, 4):
         wait_field(4, part).wait_send()
+    passed_on(0, first_crosses)
+    passed_on(1, second_crosses)
     part = grid_orb.at[pl.ds(0, 125 * 2)]
     remote(part, part, many_send.at[0], many_recv.at[0], partner).wait_send()
     part = grid_term.at[pl.ds(0, 127 * 2)]
@@ -484,6 +570,7 @@
             pltpu.VMEM((BANDS * 2, 8, 128), f32),
             pltpu.VMEM((BANDS, 1, BANDS), f32),
             pltpu.VMEM((BANDS, 1, BANDS), f32),
+            pltpu.VMEM((2, RELAYED, *TILED[1:]), f32),
             pltpu.SemaphoreType.DMA((6,)),
             pltpu.SemaphoreType.DMA((2,)),
             pltpu.SemaphoreType.DMA((2,)),
@@ -492,6 +579,8 @@
             pltpu.SemaphoreType.DMA((3,)),
             pltpu.SemaphoreType.DMA((3,)),
             pltpu.SemaphoreType.REGULAR((7,)),
+            pltpu.SemaphoreType.DMA((2,)),
+            pltpu.SemaphoreType.DMA((2,)),
         ],
         compiler_params=pltpu.CompilerParams(
             collective_id=0, has_side_effects=True, vmem_limit_bytes=62 * 1024 * 1024 + 768 * 1024

time: 71 us -> 65.5 us (0.923)
  Pallas kernels: 70.3 us -> 64.7 us
    pallas_call x1, Pallas kernels: 68.8 us -> 63.2 us  [local(): pl.pallas_call(kernel, out_shape=(pltpu.VMEM(TILED, f32), pltpu.VMEM((1,...]
where the time goes in v4:
time: 65.5 us; the launch traced here: 65.4 us
  Pallas kernels  64.7 us (99%)
    pallas_call x1, Pallas kernels, local(): pl.pallas_call(kernel, out_shape=(pltpu.VMEM(TILED, f32), pltpu.VMEM((1,...  63.2 us
    pallas_call x1, Pallas kernels, local(): pl.pallas_call(finish, out_shape=(jax.ShapeDtypeStruct(TILED, f32), jax.S...  1.49 us

profile of v4, /device:TPU:1, one launch (start us, length us, event | category | flops | bytes accessed | tf_op | source)
XLA Modules:
  0.0 65.4 jit_solution(1878227971806079503)
XLA Ops:
  0.6 63.2 %exchange.1 = (f32[8,32,8,128]{3,2,1,0:T(8,128)S(1)}, f32[1,128]{1,0:T(1,128)S(1)}) custom-call(f32[8,32,8,128]{3,2,1,0:T(8,128)} %bitcast.6, f32[32]{0:T(128)} %kv.1, s32[64,4096]{1,0:T(8,128)} %shell.1, bf16[64,192]{1,0:T(8,128)(2,1)} %constant.8.clone.left_in, f32[64,256]{1,0:T(8,128)} %constant.9.clone.four_in, f32[64,256]{1,0:T(8,128)} %constant.10.clone.forward_in, ...), custom_call_target="tpu_custom_call" | custom-call | tf_op jit(solution)/shard_map/exchange/pallas_call | solution.py:557
  63.9 1.5 %finish.1 = (f32[8,32,8,128]{3,2,1,0:T(8,128)}, f32[1,128]{1,0:T(1,128)}) custom-call(f32[8,32,8,128]{3,2,1,0:T(8,128)S(1)} %get-tuple-element.6.total, f32[1,128]{1,0:T(1,128)S(1)} %get-tuple-element.7.margin), custom_call_target="tpu_custom_call" | custom-call | tf_op jit(solution)/shard_map/finish/pallas_call | solution.py:595

commit v5 on v4

--- a/solution.py
+++ b/solution.py
@@ -13,7 +13,6 @@
 BANDS = 128
 TILES = 16
 SENT_TOGETHER = 4
-RELAYED = 2
 TILED = (8, 32, 8, 128)
 SHIFTS = sorted(
     ((dz, dy) for dz in range(4) for dy in range(4)),
@@ -172,9 +171,7 @@
     load.start()
 
     meetings = [partner]
-    neighbours = [first, second] + [
-        lax.rem(me + offset, BANDS) for offset in (6, 8, BANDS - 8, BANDS - 6)
-    ]
+    neighbours = [first, second, lax.rem(me + 8, BANDS), lax.rem(me + BANDS - 8, BANDS)]
     for scale in (2, 8, 32):
         here = lax.rem(me // scale, 4)
         base = me - here * scale
@@ -198,72 +195,56 @@
     to_partner = remote(fields.at[0], fields.at[1], send_sem.at[0], recv_sem.at[0], partner)
     forward_on = remote(fields.at[2], fields.at[3], send_sem.at[1], recv_sem.at[1], partner)
 
-    def send_field(slot, part, phase, device, below, crosses, relay_device):
-        start = 2 * lax.rem(device // 2, 4) - below + 8
-
-        def direct(i):
+    def send_groups(source, target, device_x, below, send, recv, part, device):
+        start = 2 * device_x - below + 8
+        for i in range(8):
             group = lax.rem(start + i, 8)
             index = part if i < 3 else part + 1
-            remote(
-                fields.at[0, group], fields.at[slot, group],
-                part_send.at[index], part_recv.at[index], device,
-            ).start()
-
-        @pl.when(crosses)
+            remote(source(i, group), target(i, group), send(index), recv(index), device).start()
+
+    def send_field(slot, part, device, below):
+        send_groups(
+            lambda i, group: fields.at[0, group], lambda i, group: fields.at[slot, group],
+            lax.rem(device // 2, 4), below,
+            lambda index: part_send.at[index], lambda index: part_recv.at[index],
+            part, device,
+        )
+
+    second_crosses = x == 3 - 3 * core
+
+    def send_ahead():
+        send_groups(
+            lambda i, group: fields.at[0, group], lambda i, group: relay.at[i],
+            lax.rem(second // 2, 4), core,
+            lambda index: part_send.at[index], lambda index: relay_recv.at[index - 2],
+            2, lax.rem(me + 8 - 16 * core + BANDS, BANDS),
+        )
+
+    def pass_on():
+        up = x // 3
+        device = lax.rem(me + 6 - 12 * up + BANDS, BANDS)
+        for part, groups in ((0, range(3)), (1, range(3, 8))):
+            ref = relay.at[pl.ds(0, len(groups))]
+            remote(ref, ref, relay_send, relay_recv.at[part], partner).wait_recv()
+            for i in groups:
+                remote(
+                    relay.at[i],
+                    fields.at[4, lax.rem(2 * (3 - 3 * up) - core + 8 + i, 8)],
+                    relay_send, part_recv.at[2 + part], device,
+                ).start()
+
+    def passed_on():
+        @pl.when(second_crosses)
         def _():
-            for i in range(RELAYED):
-                remote(
-                    fields.at[0, lax.rem(start + 8 - RELAYED + i, 8)],
-                    relay.at[phase, i],
-                    part_send.at[part + 1], relay_recv.at[phase], relay_device,
-                ).start()
-
-        for i in range(8 - RELAYED):
-            direct(i)
-
-        @pl.when(jnp.logical_not(crosses))
-        def _():
-            for i in range(8 - RELAYED, 8):
-                direct(i)
-
-    def pass_on(slot, part, phase, crosses):
-        @pl.when(crosses)
-        def _():
-            up = x // 3
-            device = lax.rem(me + 6 - 12 * up + BANDS, BANDS)
-            below = (1 - core) if phase == 0 else core
-            start = 2 * (3 - 3 * up) - below + 8
-            for i in range(RELAYED):
-                ref = relay.at[phase, pl.ds(0, RELAYED)]
-                if i == 0:
-                    remote(
-                        ref, ref, relay_send.at[phase], relay_recv.at[phase], partner
-                    ).wait_recv()
-                remote(
-                    relay.at[phase, i],
-                    fields.at[slot, lax.rem(start + 8 - RELAYED + i, 8)],
-                    relay_send.at[phase], part_recv.at[part + 1], device,
-                ).start()
-
-    def passed_on(phase, crosses):
-        @pl.when(crosses)
-        def _():
-            ref = relay.at[phase, pl.ds(0, RELAYED)]
-            remote(
-                ref, ref, relay_send.at[phase], relay_recv.at[phase], partner
-            ).wait_send()
+            remote(relay, relay, relay_send, relay_recv.at[0], partner).wait_send()
 
     def wait_field(slot, part):
         count = 3 if part % 2 == 0 else 5
         ref = fields.at[slot, pl.ds(0, count)]
         return remote(ref, ref, part_send.at[part], part_recv.at[part], partner)
 
-    first_crosses = x == 3 * core
-    second_crosses = x == 3 - 3 * core
-    send_field(
-        2, 0, 0, first, 1 - core, first_crosses,
-        lax.rem(me - 8 + 16 * core + BANDS, BANDS),
-    )
+    send_field(2, 0, first, 1 - core)
+    pl.when(second_crosses)(send_ahead)
     to_partner.start()
 
     def send_slice(slot, orbital, owner):
@@ -373,21 +354,20 @@
         both = dot(jnp.concatenate([high, low], axis=0), w)
         return both[:GRID] + both[GRID:] + dot(high, w_rest)
 
-    def send_terms(j):
-        def one(g, carry):
-            owner = j * 8 + g
-
-            @pl.when(owner != me)
-            def _():
-                remote(
-                    total.at[g, pl.ds(j * 2, 2)],
-                    grid_term.at[pl.ds(me * 2, 2)],
-                    many_send.at[1], many_recv.at[1], owner,
-                ).start()
-
-            return carry
-
-        lax.fori_loop(0, 8, one, 0)
+    def in_plane(shift):
+        j = plane_at(*shift)
+        for dx in (2, 1, 3, 0):
+            for side in (1, 0):
+                if shift != (0, 0) or dx != 0 or side != 0:
+                    yield j * 8 + wrap4(x + dx) * 2 + lax.rem(core + side, 2)
+
+    def send_terms(shift):
+        for owner in in_plane(shift):
+            remote(
+                total.at[lax.rem(owner, 8), pl.ds(owner // 8 * 2, 2)],
+                grid_term.at[pl.ds(me * 2, 2)],
+                many_send.at[1], many_recv.at[1], owner,
+            ).start()
 
     def one_pair(it, after=None):
         last = it == 4
@@ -452,7 +432,7 @@
                         total[:, 2 * j + i] += term
             if last and start > 0:
                 for shift in SHIFTS[start - SENT_TOGETHER : start]:
-                    send_terms(plane_at(*shift))
+                    send_terms(shift)
 
     def next_step(step):
         met(step)
@@ -469,21 +449,25 @@
         {1: lambda: next_step(3), 2: lambda: next_step(4), 3: lambda: next_step(5),
          4: lambda: met(6)},
     )
-    pass_on(2, 0, 0, first_crosses)
-    send_near(0, me)
     to_partner.wait_recv()
+
+    def fetch_second():
+        for part in range(2):
+            wait_field(2, part).wait_send()
+        pl.when(second_crosses)(pass_on)
+        pl.when(jnp.logical_not(second_crosses))(lambda: send_field(4, 2, second, core))
+
     one_pair(
-        1, {2: lambda: pass_orbital(2, 0, second, wrap4(x - 1 + 2 * core), 1 - core)}
-    )
-    for part in range(2):
-        wait_field(2, part).wait_send()
-    send_field(
-        4, 2, 1, second, core, second_crosses, lax.rem(me + 8 - 16 * core + BANDS, BANDS)
+        1,
+        {1: fetch_second,
+         3: lambda: (
+             send_near(0, me),
+             pass_orbital(2, 0, second, wrap4(x - 1 + 2 * core), 1 - core),
+         )},
     )
     wait_field(2, 1).wait_recv()
     forward_on.start()
     one_pair(2)
-    pass_on(4, 2, 1, second_crosses)
     forward_on.wait_recv()
     one_pair(
         3, {2: lambda: pass_orbital(4, 2, first, wrap4(x + 1 - 2 * core), core)}
@@ -491,7 +475,7 @@
     wait_field(4, 3).wait_recv()
     one_pair(4)
     for shift in SHIFTS[16 - SENT_TOGETHER :]:
-        send_terms(plane_at(*shift))
+        send_terms(shift)
     grid_term[pl.ds(me * 2, 2)] = total[lax.rem(me, 8), pl.ds(plane * 2, 2)]
 
     def wait_many(count, buffer, index):
@@ -515,14 +499,11 @@
     for i in range(BANDS):
         gram[i] = result[i : i + 1, :]
 
-    def send_row(t, carry):
-        owner = lax.rem(me + t, BANDS)
-        remote(
-            gram.at[owner], rows.at[me], many_send.at[2], many_recv.at[2], owner
-        ).start()
-        return carry
-
-    lax.fori_loop(1, BANDS, send_row, 0)
+    for shift in SHIFTS:
+        for owner in in_plane(shift):
+            remote(
+                gram.at[owner], rows.at[me], many_send.at[2], many_recv.at[2], owner
+            ).start()
     rows[me] = gram[me]
     part = rows.at[pl.ds(0, BANDS - 1)]
     remote(part, part, many_send.at[2], many_recv.at[2], partner).wait_recv()
@@ -532,8 +513,7 @@
     forward_on.wait_send()
     for part in range(2, 4):
         wait_field(4, part).wait_send()
-    passed_on(0, first_crosses)
-    passed_on(1, second_crosses)
+    passed_on()
     part = grid_orb.at[pl.ds(0, 125 * 2)]
     remote(part, part, many_send.at[0], many_recv.at[0], partner).wait_send()
     part = grid_term.at[pl.ds(0, 127 * 2)]
@@ -570,7 +550,7 @@
             pltpu.VMEM((BANDS * 2, 8, 128), f32),
             pltpu.VMEM((BANDS, 1, BANDS), f32),
             pltpu.VMEM((BANDS, 1, BANDS), f32),
-            pltpu.VMEM((2, RELAYED, *TILED[1:]), f32),
+            pltpu.VMEM(TILED, f32),
             pltpu.SemaphoreType.DMA((6,)),
             pltpu.SemaphoreType.DMA((2,)),
             pltpu.SemaphoreType.DMA((2,)),
@@ -579,7 +559,7 @@
             pltpu.SemaphoreType.DMA((3,)),
             pltpu.SemaphoreType.DMA((3,)),
             pltpu.SemaphoreType.REGULAR((7,)),
-            pltpu.SemaphoreType.DMA((2,)),
+            pltpu.SemaphoreType.DMA,
             pltpu.SemaphoreType.DMA((2,)),
         ],
         compiler_params=pltpu.CompilerParams(

time: 65.5 us -> 62.7 us (0.957)
  Pallas kernels: 64.7 us -> 61.8 us
    pallas_call x1, Pallas kernels: 63.2 us -> 60.3 us  [local(): pl.pallas_call(kernel, out_shape=(pltpu.VMEM(TILED, f32), pltpu.VMEM((1,...]
where the time goes in v5:
time: 62.7 us; the launch traced here: 62.6 us
  Pallas kernels  61.8 us (99%)
  between operations  0.8 us (1%)
    pallas_call x1, Pallas kernels, local(): pl.pallas_call(kernel, out_shape=(pltpu.VMEM(TILED, f32), pltpu.VMEM((1,...  60.3 us
    pallas_call x1, Pallas kernels, local(): pl.pallas_call(finish, out_shape=(jax.ShapeDtypeStruct(TILED, f32), jax.S...  1.49 us

profile of v5, /device:TPU:1, one launch (start us, length us, event | category | flops | bytes accessed | tf_op | source)
XLA Modules:
  0.0 62.6 jit_solution(4203505500406856593)
XLA Ops:
  0.6 60.3 %exchange.1 = (f32[8,32,8,128]{3,2,1,0:T(8,128)S(1)}, f32[1,128]{1,0:T(1,128)S(1)}) custom-call(f32[8,32,8,128]{3,2,1,0:T(8,128)} %bitcast.6, f32[32]{0:T(128)} %kv.1, s32[64,4096]{1,0:T(8,128)} %shell.1, bf16[64,192]{1,0:T(8,128)(2,1)} %constant.8.clone.left_in, f32[64,256]{1,0:T(8,128)} %constant.9.clone.four_in, f32[64,256]{1,0:T(8,128)} %constant.10.clone.forward_in, ...), custom_call_target="tpu_custom_call" | custom-call | tf_op jit(solution)/shard_map/exchange/pallas_call | solution.py:537
  60.9 1.5 %finish.1 = (f32[8,32,8,128]{3,2,1,0:T(8,128)}, f32[1,128]{1,0:T(1,128)}) custom-call(f32[8,32,8,128]{3,2,1,0:T(8,128)S(1)} %get-tuple-element.6.total, f32[1,128]{1,0:T(1,128)S(1)} %get-tuple-element.7.margin), custom_call_target="tpu_custom_call" | custom-call | tf_op jit(solution)/shard_map/finish/pallas_call | solution.py:575

commit v6 on v5

--- a/solution.py
+++ b/solution.py
@@ -12,7 +12,7 @@
 WIDE = GRID * GRID
 BANDS = 128
 TILES = 16
-SENT_TOGETHER = 4
+SENT_TOGETHER = 2
 TILED = (8, 32, 8, 128)
 SHIFTS = sorted(
     ((dz, dy) for dz in range(4) for dy in range(4)),
@@ -150,6 +150,7 @@
     orb, kv, shell, left_in, four_in, forward_in, backward_in, total, margin,
     fields, work, screen, classes, left, four, forward, backward,
     w_high, w_low, v_high, v_low, grid_orb, grid_term, gram, rows, relay,
+    orb_high, orb_low,
     load_sem, send_sem, recv_sem, part_send, part_recv, many_send, many_recv, meet_sem,
     relay_send, relay_recv,
 ):
@@ -470,7 +471,7 @@
     one_pair(2)
     forward_on.wait_recv()
     one_pair(
-        3, {2: lambda: pass_orbital(4, 2, first, wrap4(x + 1 - 2 * core), core)}
+        3, {4: lambda: pass_orbital(4, 2, first, wrap4(x + 1 - 2 * core), core)}
     )
     wait_field(4, 3).wait_recv()
     one_pair(4)
@@ -483,18 +484,22 @@
         remote(part, part, many_send.at[index], many_recv.at[index], partner).wait_recv()
 
     wait_many(125 * 2, grid_orb, 0)
-    wait_many(127 * 2, grid_term, 1)
     def across(buffer, s):
         flat = buffer.reshape(BANDS * 16, 128)
         return jnp.concatenate(
             [flat[pl.ds(8 * i + s, BANDS, stride=16), :] for i in range(2)], axis=1
         )
 
+    for s in range(8):
+        a_high, a_low = split(across(grid_orb, s))
+        orb_high[s], orb_low[s] = a_high, a_low
+    wait_many(127 * 2, grid_term, 1)
     result = jnp.zeros((BANDS, BANDS), f32)
     for s in range(8):
-        a_high, a_low = split(across(grid_orb, s))
+        a_high, a_low = orb_high[s], orb_low[s]
         b_high, b_low = split(across(grid_term, s))
-        result += dot_t(a_high, b_high) + dot_t(a_low, b_high) + dot_t(a_high, b_low)
+        both = dot_t(jnp.concatenate([a_high, a_low], axis=0), b_high)
+        result += both[:BANDS] + both[BANDS:] + dot_t(a_high, b_low)
     result = result * (1.0 / GRID**3)
     for i in range(BANDS):
         gram[i] = result[i : i + 1, :]
@@ -551,6 +556,7 @@
             pltpu.VMEM((BANDS, 1, BANDS), f32),
             pltpu.VMEM((BANDS, 1, BANDS), f32),
             pltpu.VMEM(TILED, f32),
+            *[pltpu.VMEM((8, BANDS, 256), bf16)] * 2,
             pltpu.SemaphoreType.DMA((6,)),
             pltpu.SemaphoreType.DMA((2,)),
             pltpu.SemaphoreType.DMA((2,)),

time: 62.7 us -> 62.3 us (level)
  no operation moved by 1% of the time
where the time goes in v6:
time: 62.3 us; the launch traced here: 62.2 us
  Pallas kernels  61.4 us (99%)
  between operations  0.8 us (1%)
    pallas_call x1, Pallas kernels, local(): pl.pallas_call(kernel, out_shape=(pltpu.VMEM(TILED, f32), pltpu.VMEM((1,...  59.9 us
    pallas_call x1, Pallas kernels, local(): pl.pallas_call(finish, out_shape=(jax.ShapeDtypeStruct(TILED, f32), jax.S...  1.49 us

profile of v6, /device:TPU:1, one launch (start us, length us, event | category | flops | bytes accessed | tf_op | source)
XLA Modules:
  0.0 62.2 jit_solution(13352994466521684404)
XLA Ops:
  0.6 59.9 %exchange.1 = (f32[8,32,8,128]{3,2,1,0:T(8,128)S(1)}, f32[1,128]{1,0:T(1,128)S(1)}) custom-call(f32[8,32,8,128]{3,2,1,0:T(8,128)} %bitcast.6, f32[32]{0:T(128)} %kv.1, s32[64,4096]{1,0:T(8,128)} %shell.1, bf16[64,192]{1,0:T(8,128)(2,1)} %constant.8.clone.left_in, f32[64,256]{1,0:T(8,128)} %constant.9.clone.four_in, f32[64,256]{1,0:T(8,128)} %constant.10.clone.forward_in, ...), custom_call_target="tpu_custom_call" | custom-call | tf_op jit(solution)/shard_map/exchange/pallas_call | solution.py:542
  60.5 1.5 %finish.1 = (f32[8,32,8,128]{3,2,1,0:T(8,128)}, f32[1,128]{1,0:T(1,128)}) custom-call(f32[8,32,8,128]{3,2,1,0:T(8,128)S(1)} %get-tuple-element.6.total, f32[1,128]{1,0:T(1,128)S(1)} %get-tuple-element.7.margin), custom_call_target="tpu_custom_call" | custom-call | tf_op jit(solution)/shard_map/finish/pallas_call | solution.py:581

commit v7 on v6

--- a/solution.py
+++ b/solution.py
@@ -442,7 +442,6 @@
     def pass_orbital(slot, part, orbital, x_there, side):
         wait_field(slot, part).wait_recv()
         send_near(slot, orbital)
-        send_across(slot, orbital, x_there, side)
 
     meet(3)
     one_pair(
@@ -474,6 +473,8 @@
         3, {4: lambda: pass_orbital(4, 2, first, wrap4(x + 1 - 2 * core), core)}
     )
     wait_field(4, 3).wait_recv()
+    send_across(2, second, wrap4(x - 1 + 2 * core), 1 - core)
+    send_across(4, first, wrap4(x + 1 - 2 * core), core)
     one_pair(4)
     for shift in SHIFTS[16 - SENT_TOGETHER :]:
         send_terms(shift)

time: 62.3 us -> 62.6 us (level)
  no operation moved by 1% of the time
where the time goes in v7:
time: 62.6 us; the launch traced here: 62.5 us
  Pallas kernels  61.7 us (99%)
  between operations  0.8 us (1%)
    pallas_call x1, Pallas kernels, local(): pl.pallas_call(kernel, out_shape=(pltpu.VMEM(TILED, f32), pltpu.VMEM((1,...  60.2 us
    pallas_call x1, Pallas kernels, local(): pl.pallas_call(finish, out_shape=(jax.ShapeDtypeStruct(TILED, f32), jax.S...  1.49 us

profile of v7, /device:TPU:1, one launch (start us, length us, event | category | flops | bytes accessed | tf_op | source)
XLA Modules:
  0.0 62.5 jit_solution(8310944608506808706)
XLA Ops:
  0.6 60.2 %exchange.1 = (f32[8,32,8,128]{3,2,1,0:T(8,128)S(1)}, f32[1,128]{1,0:T(1,128)S(1)}) custom-call(f32[8,32,8,128]{3,2,1,0:T(8,128)} %bitcast.6, f32[32]{0:T(128)} %kv.1, s32[64,4096]{1,0:T(8,128)} %shell.1, bf16[64,192]{1,0:T(8,128)(2,1)} %constant.8.clone.left_in, f32[64,256]{1,0:T(8,128)} %constant.9.clone.four_in, f32[64,256]{1,0:T(8,128)} %constant.10.clone.forward_in, ...), custom_call_target="tpu_custom_call" | custom-call | tf_op jit(solution)/shard_map/exchange/pallas_call | solution.py:543
  60.8 1.5 %finish.1 = (f32[8,32,8,128]{3,2,1,0:T(8,128)}, f32[1,128]{1,0:T(1,128)}) custom-call(f32[8,32,8,128]{3,2,1,0:T(8,128)S(1)} %get-tuple-element.6.total, f32[1,128]{1,0:T(1,128)S(1)} %get-tuple-element.7.margin), custom_call_target="tpu_custom_call" | custom-call | tf_op jit(solution)/shard_map/finish/pallas_call | solution.py:582
